TPU v7x, 32 devices: a whole 2x2x4 slice. The times are simulated.
32 devices in a mesh: feat: 4 (over y, core), dom: 8 (over z, x).
Axes of the slice: x: 2, y: 2, z: 4, core: 2. Of those that a mesh axis runs over, the one named last changes fastest.
Arguments:
- features: bfloat16 [32768, 128], P('dom'), may hold values from -6 to 6
- w_input: bfloat16 [128, 256], P(None, 'feat'), may hold values from -0.5 to 0.5
- layer_weights: bfloat16 [4, 256, 256], replicated, may hold values from -0.375 to 0.375
- history: bfloat16 [4, 32768, 256], P(None, 'dom', 'feat'), may hold values from 0 to 2
- tile_values: bfloat16 [256, 6, 128, 128], P('dom'), may hold values from -0.21875 to 0.21875
- tile_columns: int32 [256, 6], P('dom'), may hold values from 0 to 63, as said below
- send_rows: int32 [8, 8, 512], P('dom'), may hold values from 0 to 4095
- send_counts: int32 [8, 8], P('dom'), may hold values from 0 to 512, as said below
Outputs:
- pushed: bfloat16 [4, 32768, 256], P(None, 'dom', 'feat')
- final_rows: bfloat16 [32768, 256], P('dom', 'feat')
Inputs may be any that keep to these rules, and one draw needn't show every extreme that they name: `tile_columns`: per row of tiles the first 2 entries lie below 4096 / 128 (own rows), the others at or above it (halo slots); every halo column tile of every partition is named somewhere. `send_counts`: A partition sends nothing to itself; in every draw some destination receives exactly 512 rows from every other partition.
All inputs are finite; a program needn't handle non-finite values.
Results may differ from a plain program's by a relative error of at most 0.0052.
Values may be sent and summed in bfloat16 or wider, within the bound.
A program may use at most 128 MiB of HBM per device.

v0:
```python
import math

import jax
import jax.numpy as jnp
from jax import lax
from jax.sharding import PartitionSpec as P

LAYERS = 4


ALPHA = 0.1
LAMBDA_DECAY = 0.5


def propagate(own_rows, halo_rows, values, columns, tile_size):
    slice_width = own_rows.shape[1]
    combined = jnp.concatenate([own_rows, halo_rows], axis=0)
    tile_count = combined.shape[0] // tile_size
    flat_tiles = combined.reshape(tile_count, tile_size * slice_width)
    row_tiles, per_row = columns.shape
    selector = (
        columns.reshape(row_tiles * per_row, 1) == jnp.arange(tile_count, dtype=jnp.int32)[None, :]
    ).astype(jnp.bfloat16)
    picked = jnp.dot(selector, flat_tiles, preferred_element_type=jnp.float32).astype(jnp.bfloat16)
    picked = picked.reshape(row_tiles, per_row, tile_size, slice_width)
    summed = jnp.einsum("rkab,rkbf->raf", values, picked, preferred_element_type=jnp.float32)
    return summed.reshape(own_rows.shape[0], slice_width)


def on_device(
    features, w_input, layer_weights, history, tile_values, tile_columns, send_rows, send_counts
):
    initial = jnp.maximum(
        jnp.dot(features, w_input, preferred_element_type=jnp.float32), 0.0
    ).astype(jnp.bfloat16)
    nodes_local, slice_width = initial.shape
    peer_count = send_rows.shape[1]
    slot_count = send_rows.shape[2]
    tile_size = tile_values.shape[-1]
    targets = send_rows[0]
    live_slots = (jnp.arange(slot_count)[None, :] < send_counts[0][:, None])[:, :, None]
    zero_value = jnp.zeros((), jnp.bfloat16)
    halo_list = [
        lax.all_to_all(
            jnp.where(live_slots, history[level][targets], zero_value),
            "dom",
            split_axis=0,
            concat_axis=0,
            tiled=True,
        ).reshape(peer_count * slot_count, slice_width)
        for level in range(LAYERS)
    ]
    pushed = []
    current = initial
    for layer_index in range(LAYERS):
        beta_layer = math.log(LAMBDA_DECAY / (layer_index + 1) + 1.0)
        weight = layer_weights[layer_index]
        aggregated = propagate(
            current, halo_list[layer_index], tile_values, tile_columns, tile_size
        )
        blended = ((1.0 - ALPHA) * aggregated + ALPHA * initial.astype(jnp.float32)).astype(
            jnp.bfloat16
        )
        blended = lax.optimization_barrier(blended)
        pushed.append(current)
        feat_index = lax.axis_index("feat")
        weight_cols = lax.dynamic_slice_in_dim(weight, feat_index * slice_width, slice_width, 1)
        product = jnp.dot(
            lax.all_gather(blended, "feat", axis=1, tiled=True),
            weight_cols,
            preferred_element_type=jnp.float32,
        )
        fresh = jnp.maximum(
            (1.0 - beta_layer) * blended.astype(jnp.float32) + beta_layer * product, 0.0
        )
        current = fresh.astype(jnp.bfloat16)
    return (jnp.stack(pushed), current)


def solution(mesh):
    placed = (
        P("dom", None),
        P(None, "feat"),
        P(),
        P(None, "dom", "feat"),
        P("dom", None, None, None),
        P("dom", None),
        P("dom", None, None),
        P("dom", None),
    )
    return jax.shard_map(
        on_device,
        mesh=mesh,
        in_specs=placed,
        out_specs=(P(None, "dom", "feat"), P("dom", "feat")),
        check_vma=False,
    )
```

profile of v0, /device:TPU:0, one launch (start us, length us, event | category | flops | bytes accessed | tf_op | source)
XLA Modules:
  0.0 316.9 jit_solution(15745469783871784883)
XLA Ops:
  7.2 2.8 fusion.42
  10.0 0.5 copy.80
  10.5 15.0 %gather_fusion = bf16[4096,64]{1,0:T(8,128)(2,1)} fusion(bf16[4096,64]{1,0:T(8,128)(2,1)S(1)} %bitcast.113, s32[4096]{0:T(1024)S(1)} %broadcast_clamp_fusion), kind=kCustom, calls=%fused_computation | custom fusion | bytes 1064960 | tf_op jit(solution)/shard_map/gather | solution.py:45
  25.5 1.5 copy.49
  27.1 0.5 copy.81
  27.6 15.0 %gather_fusion.1 = bf16[4096,64]{1,0:T(8,128)(2,1)} fusion(bf16[4096,64]{1,0:T(8,128)(2,1)S(1)} %bitcast.115, s32[4096]{0:T(1024)S(1)} %broadcast_clamp_fusion), kind=kCustom, calls=%fused_computation.1 | custom fusion | bytes 1064960 | tf_op jit(solution)/shard_map/gather | solution.py:45
  42.6 1.5 copy.55
  44.2 1.5 copy.82
  45.7 15.0 %gather_fusion.2 = bf16[4096,64]{1,0:T(8,128)(2,1)} fusion(bf16[4096,64]{1,0:T(8,128)(2,1)S(1)} %bitcast.116, s32[4096]{0:T(1024)S(1)} %broadcast_clamp_fusion), kind=kCustom, calls=%fused_computation.2 | custom fusion | bytes 1064960 | tf_op jit(solution)/shard_map/gather | solution.py:45
  60.7 2.4 copy.61
  63.1 1.5 copy.83
  64.6 15.0 %gather_fusion.3 = bf16[4096,64]{1,0:T(8,128)(2,1)} fusion(bf16[4096,64]{1,0:T(8,128)(2,1)S(1)} %bitcast.114, s32[4096]{0:T(1024)S(1)} %broadcast_clamp_fusion), kind=kCustom, calls=%fused_computation.3 | custom fusion | bytes 1064960 | tf_op jit(solution)/shard_map/gather | solution.py:45
  79.7 1.5 copy.67
  81.2 0.1 iota_compare_fusion.5
  81.3 2.4 broadcast_select_fusion
  83.7 7.3 %all-to-all-start = ((bf16[8,512,64]{1,2,0:T(8,128)(2,1)}), bf16[8,512,64]{1,2,0:T(8,128)(2,1)S(1)}, u32[]{:S(2)}, u32[]{:S(2)}) async-start(bf16[8,512,64]{1,2,0:T(8,128)(2,1)} %get-tuple-element.13), calls=%async_computation | async-start | bytes 1048576 | tf_op jit(solution)/shard_map/all_to_all | solution.py:44
  91.0 0.1 copy.47
  91.1 0.1 eq.8
  91.2 0.5 fusion.12
  91.7 13.7 %all-to-all-done = bf16[8,512,64]{1,2,0:T(8,128)(2,1)S(1)} async-done(((bf16[8,512,64]{1,2,0:T(8,128)(2,1)}), bf16[8,512,64]{1,2,0:T(8,128)(2,1)S(1)}, u32[]{:S(2)}, u32[]{:S(2)}) %all-to-all-start) | async-done | bytes 524320 | tf_op jit(solution)/shard_map/all_to_all | solution.py:44
  105.5 0.1 pad_maximum_fusion.1
  105.6 1.8 copy.51
  107.4 3.3 %reshape.114 = bf16[64,8192]{1,0:T(8,128)(2,1)S(1)} reshape(bf16[8192,64]{1,0:T(8,128)(2,1)} %copy.51) | data formatting | bytes 2097152 | tf_op jit(solution)/shard_map/reshape | solution.py:19
  110.7 2.7 convolution_convert_fusion.3
  113.4 9.7 %reshape.115 = bf16[32,6,128,64]{3,2,1,0:T(8,128)(2,1)} reshape(bf16[192,8192]{1,0:T(8,128)(2,1)} %convolution_convert_fusion.3) | data formatting | bytes 6291456 | tf_op jit(solution)/shard_map/reshape | solution.py:25
  123.1 6.8 %fusion.14 = f32[32,8,8,128]{3,2,1,0:T(8,128)S(1)} fusion(bf16[32,6,128,64]{3,2,1,0:T(8,128)(2,1)} %reshape.115, bf16[32,6,128,128]{3,2,1,0:T(8,128)(2,1)} %param.12), kind=kOutput, calls=%fused_computation.32 | convolution fusion | flops 402915328 | bytes 10485760 | tf_op jit(solution)/shard_map/rkab,rkbf->raf/dot_general | solution.py:26
  129.9 0.9 fusion.24
  130.8 3.8 %all-to-all-start.1 = ((bf16[8,512,64]{1,2,0:T(8,128)(2,1)}), bf16[8,512,64]{1,2,0:T(8,128)(2,1)S(1)}, u32[]{:S(2)}, u32[]{:S(2)}) async-start(bf16[8,512,64]{1,2,0:T(8,128)(2,1)} %get-tuple-element.11), calls=%async_computation.1 | async-start | bytes 1048576 | tf_op jit(solution)/shard_map/all_to_all | solution.py:44
  134.6 0.2 all-gather.7.cloned.1.call-start
  134.9 14.4 %all-to-all-done.1 = bf16[8,512,64]{1,2,0:T(8,128)(2,1)S(1)} async-done(((bf16[8,512,64]{1,2,0:T(8,128)(2,1)}), bf16[8,512,64]{1,2,0:T(8,128)(2,1)S(1)}, u32[]{:S(2)}, u32[]{:S(2)}) %all-to-all-start.1) | async-done | bytes 524320 | tf_op jit(solution)/shard_map/all_to_all | solution.py:44
  149.3 3.3 %all-gather.5.cloned.1.call-done = bf16[4096,256]{0,1:T(8,128)(2,1)} async-done(((bf16[4096,64]{0,1:T(8,128)(2,1)}), bf16[4096,256]{0,1:T(8,128)(2,1)}) %all-gather.5.cloned.1.call-update) | async-done | bytes 2097168 | tf_op jit(solution)/shard_map/all_gather | solution.py:69
  152.6 2.2 fusion.11
  154.8 0.1 pad_maximum_fusion.2
  154.9 1.8 copy.57
  156.7 3.3 %reshape.117 = bf16[64,8192]{1,0:T(8,128)(2,1)S(1)} reshape(bf16[8192,64]{1,0:T(8,128)(2,1)} %copy.57) | data formatting | bytes 2097152 | tf_op jit(solution)/shard_map/reshape | solution.py:19
  160.0 2.7 convolution_convert_fusion.2
  162.7 9.7 %reshape.118 = bf16[32,6,128,64]{3,2,1,0:T(8,128)(2,1)} reshape(bf16[192,8192]{1,0:T(8,128)(2,1)} %convolution_convert_fusion.2) | data formatting | bytes 6291456 | tf_op jit(solution)/shard_map/reshape | solution.py:25
  172.4 6.8 %fusion.16 = f32[32,8,8,128]{3,2,1,0:T(8,128)S(1)} fusion(bf16[32,6,128,64]{3,2,1,0:T(8,128)(2,1)} %reshape.118, bf16[32,6,128,128]{3,2,1,0:T(8,128)(2,1)} %param.12), kind=kOutput, calls=%fused_computation.34 | convolution fusion | flops 402915328 | bytes 10485760 | tf_op jit(solution)/shard_map/rkab,rkbf->raf/dot_general | solution.py:26
  179.2 0.9 fusion.23
  180.2 0.1 copy-done.8
  180.2 20.3 %all_to_all.20 = bf16[8,512,64]{1,2,0:T(8,128)(2,1)S(1)} all-to-all(bf16[8,512,64]{1,2,0:T(8,128)(2,1)S(1)} %copy-done.8), channel_id=1, replica_groups=mesh['feat'=4,'dom'=8] {'dom'}, dimensions={0} | all-to-all | bytes 1048576 | tf_op jit(solution)/shard_map/all_to_all | solution.py:44
  200.6 2.2 all-gather.7.cloned.1.call-done
  202.8 2.2 fusion.10
  205.0 0.1 pad_maximum_fusion.3
  205.1 1.8 copy.63
  206.9 3.3 %reshape.120 = bf16[64,8192]{1,0:T(8,128)(2,1)S(1)} reshape(bf16[8192,64]{1,0:T(8,128)(2,1)} %copy.63) | data formatting | bytes 2097152 | tf_op jit(solution)/shard_map/reshape | solution.py:19
  210.2 2.7 convolution_convert_fusion.1
  212.9 9.7 %reshape.121 = bf16[32,6,128,64]{3,2,1,0:T(8,128)(2,1)} reshape(bf16[192,8192]{1,0:T(8,128)(2,1)} %convolution_convert_fusion.1) | data formatting | bytes 6291456 | tf_op jit(solution)/shard_map/reshape | solution.py:25
  222.6 6.8 %fusion.18 = f32[32,8,8,128]{3,2,1,0:T(8,128)S(1)} fusion(bf16[32,6,128,64]{3,2,1,0:T(8,128)(2,1)} %reshape.121, bf16[32,6,128,128]{3,2,1,0:T(8,128)(2,1)} %param.12), kind=kOutput, calls=%fused_computation.36 | convolution fusion | flops 402915328 | bytes 10485760 | tf_op jit(solution)/shard_map/rkab,rkbf->raf/dot_general | solution.py:26
  229.4 0.9 fusion.22
  230.4 0.1 copy-done.7
  230.4 20.3 %all_to_all.21 = bf16[8,512,64]{1,2,0:T(8,128)(2,1)S(1)} all-to-all(bf16[8,512,64]{1,2,0:T(8,128)(2,1)S(1)} %copy-done.7), channel_id=1, replica_groups=mesh['feat'=4,'dom'=8] {'dom'}, dimensions={0} | all-to-all | bytes 1048576 | tf_op jit(solution)/shard_map/all_to_all | solution.py:44
  250.8 2.2 all-gather.9.cloned.1.call-done
  253.0 2.2 fusion.9
  255.3 1.1 pad_maximum_fusion.4
  256.4 2.7 copy.69
  259.1 4.2 %reshape.123 = bf16[64,8192]{1,0:T(8,128)(2,1)} reshape(bf16[8192,64]{1,0:T(8,128)(2,1)} %copy.69) | data formatting | bytes 2097152 | tf_op jit(solution)/shard_map/reshape | solution.py:19
  263.3 3.9 %convolution_convert_fusion = bf16[192,8192]{1,0:T(8,128)(2,1)} fusion(bf16[64,8192]{1,0:T(8,128)(2,1)} %reshape.123, s32[192]{0:T(256)S(1)} %eq.8), kind=kOutput, calls=%fused_computation.4 | convolution fusion | flops 202911744 | bytes 4195072 | tf_op jit(solution)/shard_map/dot_general | solution.py:24
  267.3 9.7 %reshape.124 = bf16[32,6,128,64]{3,2,1,0:T(8,128)(2,1)} reshape(bf16[192,8192]{1,0:T(8,128)(2,1)} %convolution_convert_fusion) | data formatting | bytes 6291456 | tf_op jit(solution)/shard_map/reshape | solution.py:25
  276.9 6.8 %fusion.20 = f32[32,8,8,128]{3,2,1,0:T(8,128)S(1)} fusion(bf16[32,6,128,64]{3,2,1,0:T(8,128)(2,1)} %reshape.124, bf16[32,6,128,128]{3,2,1,0:T(8,128)(2,1)} %param.12), kind=kOutput, calls=%fused_computation.38 | convolution fusion | flops 402915328 | bytes 10485760 | tf_op jit(solution)/shard_map/rkab,rkbf->raf/dot_general | solution.py:26
  283.7 0.9 fusion.21
  284.7 2.7 pad_maximum_fusion
  287.4 19.9 %all-gather.11.cloned.1.call-done = bf16[4096,256]{0,1:T(8,128)(2,1)} async-done(((bf16[4096,64]{0,1:T(8,128)(2,1)}), bf16[4096,256]{0,1:T(8,128)(2,1)}) %all-gather.11.cloned.1.call-update) | async-done | bytes 2097168 | tf_op jit(solution)/shard_map/all_gather | solution.py:69
  307.4 3.0 fusion.8
  (41 shorter events, 0.5 us)
Async XLA Ops:
  7.2 84.1 %copy-start = (bf16[4096,128]{1,0:T(8,128)(2,1)S(1)}, bf16[4096,128]{1,0:T(8,128)(2,1)}, u32[]{:S(2)}) copy-start(bf16[4096,128]{1,0:T(8,128)(2,1)} %param.8) | copy-start | bytes 3145732
  7.2 3.3 %copy-start.11 = (s32[1,8,512]{2,1,0:T(8,128)S(1)}, s32[1,8,512]{2,1,0:T(8,128)}, u32[]{:S(2)}) copy-start(s32[1,8,512]{2,1,0:T(8,128)} %param.14) | copy-start | bytes 49156
  64.6 16.6 %copy-start.13 = (s32[1,8]{1,0:T(1,128)S(1)}, s32[1,8]{1,0:T(1,128)}, u32[]{:S(2)}) copy-start(s32[1,8]{1,0:T(1,128)} %param.15) | copy-start | bytes 100
  81.3 9.7 %copy-start.12 = (s32[32,6]{0,1:T(8,128)S(1)}, s32[32,6]{0,1:T(8,128)}, u32[]{:S(2)}) copy-start(s32[32,6]{0,1:T(8,128)} %param.13) | copy-start | bytes 2308
  81.3 9.9 %copy-start.10 = (bf16[128,64]{0,1:T(8,128)(2,1)S(1)}, bf16[128,64]{0,1:T(8,128)(2,1)}, u32[]{:S(2)}) copy-start(bf16[128,64]{0,1:T(8,128)(2,1)} %param.9) | copy-start | bytes 49156
  83.7 21.8 %all-to-all-start = ((bf16[8,512,64]{1,2,0:T(8,128)(2,1)}), bf16[8,512,64]{1,2,0:T(8,128)(2,1)S(1)}, u32[]{:S(2)}, u32[]{:S(2)}) async-start(bf16[8,512,64]{1,2,0:T(8,128)(2,1)} %get-tuple-element.13), calls=%async_computation | async-start | bytes 1048576 | tf_op jit(solution)/shard_map/all_to_all | solution.py:44
  91.0 61.6 %all-gather.5.cloned.1.call-start = ((), (), s32[]{:S(2)}) async-start(), calls=%async_computation.4 | async-start | bytes 2621440 | tf_op jit(solution)/shard_map/all_gather | solution.py:69
  129.8 5.0 %copy-start.9 = (bf16[4,256,256]{2,1,0:T(8,128)(2,1)S(1)}, bf16[4,256,256]{2,1,0:T(8,128)(2,1)}, u32[]{:S(2)}) copy-start(bf16[4,256,256]{2,1,0:T(8,128)(2,1)} %param.10) | copy-start | bytes 1572868
  130.8 21.8 %copy-start.2 = (bf16[4096,64]{0,1:T(8,128)(2,1)S(1)}, bf16[4096,64]{0,1:T(8,128)(2,1)}, u32[]{:S(2)}) copy-start(bf16[4096,64]{0,1:T(8,128)(2,1)} %fusion.24) | copy-start | bytes 1572868
  130.8 18.4 %all-to-all-start.1 = ((bf16[8,512,64]{1,2,0:T(8,128)(2,1)}), bf16[8,512,64]{1,2,0:T(8,128)(2,1)S(1)}, u32[]{:S(2)}, u32[]{:S(2)}) async-start(bf16[8,512,64]{1,2,0:T(8,128)(2,1)} %get-tuple-element.11), calls=%async_computation.1 | async-start | bytes 1048576 | tf_op jit(solution)/shard_map/all_to_all | solution.py:44
  134.6 68.2 %all-gather.7.cloned.1.call-start = ((), (), s32[]{:S(2)}) async-start(), calls=%async_computation.5 | async-start | bytes 2621440 | tf_op jit(solution)/shard_map/all_gather | solution.py:69
  179.2 1.1 copy-start.8
  180.1 22.7 %copy-start.5 = (bf16[4096,64]{0,1:T(8,128)(2,1)S(1)}, bf16[4096,64]{0,1:T(8,128)(2,1)}, u32[]{:S(2)}) copy-start(bf16[4096,64]{0,1:T(8,128)(2,1)} %fusion.23) | copy-start | bytes 1572868
  180.1 72.9 %all-gather.9.cloned.1.call-start = ((), (), s32[]{:S(2)}) async-start(), calls=%async_computation.6 | async-start | bytes 2621440 | tf_op jit(solution)/shard_map/all_gather | solution.py:69
  229.4 1.1 copy-start.7
  230.3 22.7 %copy-start.3 = (bf16[4096,64]{0,1:T(8,128)(2,1)S(1)}, bf16[4096,64]{0,1:T(8,128)(2,1)}, u32[]{:S(2)}) copy-start(bf16[4096,64]{0,1:T(8,128)(2,1)} %fusion.22) | copy-start | bytes 1572868
  230.3 77.0 %all-gather.11.cloned.1.call-start = ((), (), s32[]{:S(2)}) async-start(), calls=%async_computation.7 | async-start | bytes 2621440 | tf_op jit(solution)/shard_map/all_gather | solution.py:69
  255.3 3.9 %copy-start.6 = (bf16[4096,64]{0,1:T(8,128)(2,1)}, bf16[4096,64]{0,1:T(8,128)(2,1)S(1)}, u32[]{:S(2)}) copy-start(bf16[4096,64]{0,1:T(8,128)(2,1)S(1)} %fusion.9) | copy-start | bytes 1572868
  284.7 22.7 %copy-start.4 = (bf16[4096,64]{0,1:T(8,128)(2,1)S(1)}, bf16[4096,64]{0,1:T(8,128)(2,1)}, u32[]{:S(2)}) copy-start(bf16[4096,64]{0,1:T(8,128)(2,1)} %fusion.21) | copy-start | bytes 1572868
  284.7 25.7 %copy-start.1 = (bf16[4096,128]{1,0:T(8,128)(2,1)S(1)}, bf16[4096,128]{1,0:T(8,128)(2,1)}, u32[]{:S(2)}) copy-start(bf16[4096,128]{1,0:T(8,128)(2,1)} %param.8) | copy-start | bytes 3145732
Sparse Core Ops, SparseCore 0:
  130.9 21.6 all-gather.4
  180.2 22.5 all-gather.6
  230.4 22.5 all-gather.8
  284.8 22.5 all-gather.10
where the time goes:
time: 319 us; the launch traced here: 317 us
  local copies, waits for them, and re-layouts  135 us (42%)
  waiting for transfers between devices  55.9 us (18%)
  matrix products  49.3 us (15%)
  blocking collectives  40.6 us (13%)
  between operations  14.1 us (4%)
  starting transfers between devices  11.4 us (4%)
  other arithmetic  10.3 us (3%)
    gather x8, local copies, waits for them, and re-layouts, on_device(): history[level][targets]  67.2 us
    all_to_all x2, blocking collectives, on_device(): lax.all_to_all(jnp.where(live_slots, history[level][targets], zero_value)...  40.6 us
    reshape x4, local copies, waits for them, and re-layouts, propagate(): picked = picked.reshape(row_tiles, per_row, tile_size, slice_width)  38.7 us
    all_to_all x2, waiting for transfers between devices, on_device(): lax.all_to_all(jnp.where(live_slots, history[level][targets], zero_value)...  28.1 us
    all_gather x4, waiting for transfers between devices, on_device(): lax.all_gather(blended, 'feat', axis=1, tiled=True)  27.7 us
    dot_general x4, matrix products, propagate(): jnp.einsum('rkab,rkbf->raf', values, picked, preferred_element_type=jnp.f...  27.1 us
    reshape x4, local copies, waits for them, and re-layouts, propagate(): flat_tiles = combined.reshape(tile_count, tile_size * slice_width)  14.1 us
    dot_general x4, matrix products, propagate(): jnp.dot(selector, flat_tiles, preferred_element_type=jnp.float32)  12.1 us
  transfers between devices with their start and end apart: 6, of which 6 were waited for; matrix products, arithmetic and copies ran while one was open for 1% of the time, Pallas kernels for 0%

commit v1 on v0

v1 whole, which is shorter than its diff:
```python
import functools
import math

import jax
import jax.numpy as jnp
from jax import lax
from jax.experimental import pallas as pl
from jax.experimental.pallas import tpu as pltpu
from jax.sharding import PartitionSpec as P

ALPHA = 0.1
LAMBDA_DECAY = 0.5
CORES = 2
OWN_TILES = 2
MESH = pl.DeviceIdType.MESH
NT = (((1,), (1,)), ((), ()))


def kernel(
    doms, feats, layers, tile, columns_ref, counts_ref, rows_ref, history_hbm, features_hbm,
    w_ref, weights_ref, values_hbm, pushed_hbm, final_hbm, *scratch
):
    halos = scratch[:layers]
    (history, features, w_all, weights_t, values, outgoing, initial, ping, pong,
     load_sem, w_send, w_recv, z_send, z_recv, y_send, y_recv, c_send, c_recv, out_sem) = scratch[layers:]
    width = w_ref.shape[0]
    nodes = history.shape[1]
    cap = rows_ref.shape[1]
    row_tiles, per_row = values.shape[0], values.shape[1]
    chips = feats // CORES
    dom = lax.axis_index("dom")
    feat = lax.axis_index("feat")
    chip, core = feat // CORES, feat % CORES
    sibling = chip * CORES + (1 - core)

    loads = [
        pltpu.make_async_copy(history_hbm, history, load_sem.at[0]),
        pltpu.make_async_copy(features_hbm, features, load_sem.at[1]),
        pltpu.make_async_copy(values_hbm, values, load_sem.at[2]),
    ]
    for load in loads:
        load.start()

    barrier = pltpu.get_barrier_semaphore()
    for step in range(1, doms):
        pl.semaphore_signal(
            barrier, inc=1, device_id={"dom": lax.rem(dom + step, doms)}, device_id_type=MESH
        )
    for step in range(1, feats):
        pl.semaphore_signal(
            barrier, inc=1, device_id={"feat": lax.rem(feat + step, feats)}, device_id_type=MESH
        )

    def slice_rows(index):
        return pl.ds(pl.multiple_of(index * width, width), width)

    blocks = cap // tile

    def block_tiles(source):
        return pl.ds(source * blocks, blocks)

    def w_copy(step):
        return pltpu.make_async_remote_copy(
            src_ref=w_ref,
            dst_ref=w_all.at[slice_rows(feat)],
            send_sem=w_send.at[step],
            recv_sem=w_recv.at[step],
            device_id={"feat": lax.rem(feat + step, feats)},
            device_id_type=MESH,
        )

    def z_copy(level, step):
        dest = lax.rem(dom + step, doms)
        return pltpu.make_async_remote_copy(
            src_ref=outgoing.at[step, :, pl.ds(level * width, width)],
            dst_ref=halos[level].at[block_tiles(dom), slice_rows(feat)],
            send_sem=z_send.at[level, step],
            recv_sem=z_recv.at[level, step],
            device_id={"dom": dest},
            device_id_type=MESH,
        )

    def y_copy(level, step, hop):
        source = lax.rem(dom + doms - step, doms)
        block = halos[level].at[block_tiles(source), slice_rows(feat)]
        return pltpu.make_async_remote_copy(
            src_ref=block,
            dst_ref=block,
            send_sem=y_send.at[level, step, hop],
            recv_sem=y_recv.at[level, step, hop],
            device_id={"feat": lax.rem(chip + hop, chips) * CORES + core},
            device_id_type=MESH,
        )

    def c_copy(level, step, hop):
        source = lax.rem(dom + doms - step, doms)
        owner = lax.rem(chip + chips - hop, chips) * CORES + core
        block = halos[level].at[block_tiles(source), slice_rows(owner)]
        return pltpu.make_async_remote_copy(
            src_ref=block,
            dst_ref=block,
            send_sem=c_send.at[level, step, hop],
            recv_sem=c_recv.at[level, step, hop],
            device_id={"feat": sibling},
            device_id_type=MESH,
        )

    def gather(step):
        dest = lax.rem(dom + step, doms)
        part = min(cap, 256)
        for begin in range(0, cap, part):
            slots = begin + lax.broadcasted_iota(jnp.int32, (1, part), 1)
            rows = rows_ref[pl.ds(dest, 1), pl.ds(begin, part)]
            rows = jnp.where(slots < counts_ref[0, dest], rows, -1)
            nodes_iota = lax.broadcasted_iota(jnp.int32, (nodes, part), 0)
            onehot = jnp.where(nodes_iota == rows, 1.0, 0.0).astype(jnp.bfloat16)
            picked = jnp.dot(history[...], onehot, preferred_element_type=jnp.float32)
            picked = picked.astype(jnp.bfloat16)
            for offset in range(0, part, tile):
                outgoing[step, (begin + offset) // tile] = picked[:, offset : offset + tile]

    loads[0].wait()
    gather(1)
    pl.semaphore_wait(barrier, doms + feats - 2)
    for step in range(1, feats):
        w_copy(step).start()
    z_copy(0, 1).start()

    def gather_step(step, carry):
        gather(step)
        z_copy(0, step).start()
        return carry

    lax.fori_loop(2, doms, gather_step, 0)
    for level in range(1, layers):

        def send_step(step, carry, level=level):
            z_copy(level, step).start()
            return carry

        lax.fori_loop(1, doms, send_step, 0)

    for level in range(layers):
        halos[level][block_tiles(dom)] = jnp.zeros((blocks, width * feats, tile), jnp.bfloat16)
        weights_t[level] = weights_ref[level].astype(jnp.float32).T.astype(jnp.bfloat16)

    w_all[slice_rows(feat), :] = w_ref[...]
    for step in range(1, feats):
        w_copy(step).wait_recv()
    loads[1].wait()

    def initial_step(index, carry):
        part = pl.ds(pl.multiple_of(index * cap, cap), cap)
        product = lax.dot_general(
            w_all[...], features[part, :], NT, preferred_element_type=jnp.float32
        )
        product = jnp.maximum(product, 0.0).astype(jnp.bfloat16)
        for offset in range(blocks):
            initial[index * blocks + offset] = product[:, offset * tile : (offset + 1) * tile]
        return carry

    lax.fori_loop(0, nodes // cap, initial_step, 0)
    loads[2].wait()

    def push(level, buffer):
        target = pushed_hbm.at[level] if level < layers else final_hbm
        return pltpu.make_async_copy(buffer.at[:, slice_rows(feat)], target, out_sem.at[level])

    states = [initial] + [ping if index % 2 == 0 else pong for index in range(layers)]
    push(0, initial).start()
    group = row_tiles // doms

    def layer_group(layer, index):
        beta = math.log(LAMBDA_DECAY / (layer + 1) + 1.0)
        current, following, halo = states[layer], states[layer + 1], halos[layer]
        pieces = []
        for offset in range(group):
            row = index * group + offset
            picked = []
            for k in range(per_row):
                column = columns_ref[row, k]
                if k < OWN_TILES:
                    picked.append(current[column])
                else:
                    picked.append(halo[column])
            total = lax.dot_general(
                jnp.concatenate(picked, axis=1),
                jnp.concatenate([values[row, k] for k in range(per_row)], axis=1),
                NT,
                preferred_element_type=jnp.float32,
            )
            pieces.append(total)
        first = index * group
        start = jnp.concatenate([initial[first + offset] for offset in range(group)], axis=1)
        aggregated = jnp.concatenate(pieces, axis=1) if group > 1 else pieces[0]
        blended = (
            (1.0 - ALPHA) * aggregated + ALPHA * start.astype(jnp.float32)
        ).astype(jnp.bfloat16)
        product = jnp.dot(weights_t[layer], blended, preferred_element_type=jnp.float32)
        fresh = jnp.maximum((1.0 - beta) * blended.astype(jnp.float32) + beta * product, 0.0)
        fresh = fresh.astype(jnp.bfloat16)
        for offset in range(group):
            following[first + offset] = fresh[:, offset * tile : (offset + 1) * tile]

    for level in range(layers + 1):
        layer = level - 1
        if layer >= 2:
            push(layer - 1, states[layer - 1]).wait()
        if layer >= 0:
            layer_group(layer, 0)

        def arrive(step, carry, level=level, layer=layer):
            if level < layers:
                z_copy(level, step).wait_recv()
                for hop in range(1, chips):
                    y_copy(level, step, hop).start()
                c_copy(level, step, 0).start()
            if layer >= 0:
                layer_group(layer, step)
            return carry

        lax.fori_loop(1, doms, arrive, 0)
        if layer >= 0:
            push(layer + 1, states[layer + 1]).start()
        if level < layers:

            def relay(step, carry, level=level):
                for hop in range(1, chips):
                    y_copy(level, step, hop).wait_recv()
                    c_copy(level, step, hop).start()
                return carry

            lax.fori_loop(1, doms, relay, 0)

            def settle(step, carry, level=level):
                for hop in range(chips):
                    c_copy(level, step, hop).wait_recv()
                return carry

            lax.fori_loop(1, doms, settle, 0)

    for step in range(1, feats):
        w_copy(step).wait_send()
    for level in range(layers):

        def drain(step, carry, level=level):
            z_copy(level, step).wait_send()
            for hop in range(chips):
                c_copy(level, step, hop).wait_send()
            for hop in range(1, chips):
                y_copy(level, step, hop).wait_send()
            return carry

        lax.fori_loop(1, doms, drain, 0)
    waited = set(range(1, layers - 1))
    for level in range(layers + 1):
        if level not in waited:
            push(level, states[level]).wait()


def on_device(doms, feats, features, w_input, layer_weights, history, tile_values, tile_columns, send_rows, send_counts):
    layers, nodes, width = history.shape
    row_tiles, per_row, tile, _ = tile_values.shape
    cap = send_rows.shape[2]
    hidden = width * feats
    chips = feats // CORES
    any_spec = pl.BlockSpec(memory_space=pl.ANY)
    vmem = pl.BlockSpec(memory_space=pltpu.VMEM)
    smem = pl.BlockSpec(memory_space=pltpu.SMEM)
    bf16 = jnp.bfloat16
    dma = pltpu.SemaphoreType.DMA
    pushed, final = pl.pallas_call(
        functools.partial(kernel, doms, feats, layers, tile),
        out_shape=(
            jax.ShapeDtypeStruct((layers, row_tiles, width, tile), bf16),
            jax.ShapeDtypeStruct((row_tiles, width, tile), bf16),
        ),
        in_specs=[smem, smem, vmem, any_spec, any_spec, vmem, vmem, any_spec],
        out_specs=(any_spec, any_spec),
        scratch_shapes=[pltpu.VMEM((doms * cap // tile, hidden, tile), bf16) for _ in range(layers)] + [
            pltpu.VMEM((layers * width, nodes), bf16),
            pltpu.VMEM(features.shape, bf16),
            pltpu.VMEM((hidden, features.shape[1]), bf16),
            pltpu.VMEM((layers, hidden, hidden), bf16),
            pltpu.VMEM(tile_values.shape, bf16),
            pltpu.VMEM((doms, cap // tile, layers * width, tile), bf16),
            pltpu.VMEM((row_tiles, hidden, tile), bf16),
            pltpu.VMEM((row_tiles, hidden, tile), bf16),
            pltpu.VMEM((row_tiles, hidden, tile), bf16),
            dma((3,)),
            dma((feats,)),
            dma((feats,)),
            dma((layers, doms)),
            dma((layers, doms)),
            dma((layers, doms, chips)),
            dma((layers, doms, chips)),
            dma((layers, doms, chips)),
            dma((layers, doms, chips)),
            dma((layers + 1,)),
        ],
        compiler_params=pltpu.CompilerParams(
            collective_id=0, has_side_effects=True, vmem_limit_bytes=67043328
        ),
    )(
        jnp.where(jnp.arange(per_row) < OWN_TILES, tile_columns, tile_columns - row_tiles),
        send_counts,
        send_rows[0],
        jnp.swapaxes(history, 1, 2).reshape(layers * width, nodes),
        features,
        w_input.T,
        layer_weights,
        tile_values,
    )
    pushed = jnp.transpose(pushed, (0, 1, 3, 2)).reshape(layers, nodes, width)
    return pushed, jnp.transpose(final, (0, 2, 1)).reshape(nodes, width)


def solution(mesh):
    placed = (
        P("dom", None),
        P(None, "feat"),
        P(),
        P(None, "dom", "feat"),
        P("dom", None, None, None),
        P("dom", None),
        P("dom", None, None),
        P("dom", None),
    )
    return jax.shard_map(
        functools.partial(on_device, mesh.shape["dom"], mesh.shape["feat"]),
        mesh=mesh,
        in_specs=placed,
        out_specs=(P(None, "dom", "feat"), P("dom", "feat")),
        check_vma=False,
    )
```

time: 319 us -> 91.7 us (0.29)
  the two profiles are of different devices: /device:TPU:0 before, /device:TPU:9 now
where the time goes in v1:
time: 91.7 us; the launch traced here: 91.5 us
  Pallas kernels  85.3 us (93%)
  local copies, waits for them, and re-layouts  4.93 us (5%)
    pallas_call x1, Pallas kernels, on_device(): pl.pallas_call(functools.partial(kernel, doms, feats, layers, tile), out_...  85.3 us
    reshape x1, local copies, waits for them, and re-layouts, on_device(): pushed = jnp.transpose(pushed, (0, 1, 3, 2)).reshape(layers, nodes, width)  3.29 us

profile of v1, /device:TPU:9, one launch (start us, length us, event | category | flops | bytes accessed | tf_op | source)
XLA Modules:
  0.0 91.5 jit_solution(4903907401976684332)
XLA Ops:
  0.6 0.8 copy.13
  1.4 0.6 add_select_fusion.columns_ref
  2.0 85.3 %shard_map.95 = (bf16[4,32,64,128]{3,2,1,0:T(8,128)(2,1)}, bf16[32,64,128]{2,1,0:T(8,128)(2,1)}) custom-call(s32[32,6]{1,0:T(8,128)} %add_select_fusion.columns_ref, s32[1,8]{1,0:T(1,128)} %counts_ref.1, s32[8,512]{1,0:T(8,128)} %bitcast.18, bf16[256,4096]{1,0:T(8,128)(2,1)} %bitcast.17, bf16[4096,128]{1,0:T(8,128)(2,1)} %features_hbm.1, ...), custom_call_target="tpu_custom_call" | custom-call | tf_op jit(solution)/shard_map/pallas_call | solution.py:272
  87.4 0.0 copy-start
  87.4 3.3 %copy_bitcast_fusion = bf16[4,4096,64]{1,2,0:T(8,128)(2,1)} fusion(bf16[4,32,64,128]{3,2,1,0:T(8,128)(2,1)} %get-tuple-element.4), kind=kLoop, calls=%fused_computation | loop fusion | bytes 4194304 | tf_op jit(solution)/shard_map/reshape | solution.py:314
  90.7 0.0 copy-done
  90.7 0.9 copy_bitcast_fusion.1
  (1 shorter events, 0.0 us)
Async XLA Ops:
  87.4 3.3 %copy-start = (bf16[32,64,128]{2,1,0:T(8,128)(2,1)S(1)}, bf16[32,64,128]{2,1,0:T(8,128)(2,1)}, u32[]{:S(2)}) copy-start(bf16[32,64,128]{2,1,0:T(8,128)(2,1)} %get-tuple-element.5) | copy-start | bytes 1572868

commit v2 on v1

--- a/solution.py
+++ b/solution.py
@@ -12,6 +12,7 @@
 LAMBDA_DECAY = 0.5
 CORES = 2
 OWN_TILES = 2
+LAG = 2
 MESH = pl.DeviceIdType.MESH
 NT = (((1,), (1,)), ((), ()))
 
@@ -56,6 +57,14 @@
 
     blocks = cap // tile
 
+    def partner(step):
+        flips, bit = doms - step, 1
+        dest = dom
+        while bit < doms:
+            dest = dest + lax.rem(flips // bit, 2) * (bit - 2 * bit * lax.rem(dom // bit, 2))
+            bit *= 2
+        return dest
+
     def block_tiles(source):
         return pl.ds(source * blocks, blocks)
 
@@ -70,7 +79,7 @@
         )
 
     def z_copy(level, step):
-        dest = lax.rem(dom + step, doms)
+        dest = partner(step)
         return pltpu.make_async_remote_copy(
             src_ref=outgoing.at[step, :, pl.ds(level * width, width)],
             dst_ref=halos[level].at[block_tiles(dom), slice_rows(feat)],
@@ -81,7 +90,7 @@
         )
 
     def y_copy(level, step, hop):
-        source = lax.rem(dom + doms - step, doms)
+        source = partner(step)
         block = halos[level].at[block_tiles(source), slice_rows(feat)]
         return pltpu.make_async_remote_copy(
             src_ref=block,
@@ -93,7 +102,7 @@
         )
 
     def c_copy(level, step, hop):
-        source = lax.rem(dom + doms - step, doms)
+        source = partner(step)
         owner = lax.rem(chip + chips - hop, chips) * CORES + core
         block = halos[level].at[block_tiles(source), slice_rows(owner)]
         return pltpu.make_async_remote_copy(
@@ -106,7 +115,7 @@
         )
 
     def gather(step):
-        dest = lax.rem(dom + step, doms)
+        dest = partner(step)
         part = min(cap, 256)
         for begin in range(0, cap, part):
             slots = begin + lax.broadcasted_iota(jnp.int32, (1, part), 1)
@@ -148,27 +157,23 @@
     for step in range(1, feats):
         w_copy(step).wait_recv()
     loads[1].wait()
-
-    def initial_step(index, carry):
-        part = pl.ds(pl.multiple_of(index * cap, cap), cap)
+    group = row_tiles // doms
+
+    def initial_group(index):
+        span = group * tile
+        part = pl.ds(pl.multiple_of(index * span, span), span)
         product = lax.dot_general(
             w_all[...], features[part, :], NT, preferred_element_type=jnp.float32
         )
         product = jnp.maximum(product, 0.0).astype(jnp.bfloat16)
-        for offset in range(blocks):
-            initial[index * blocks + offset] = product[:, offset * tile : (offset + 1) * tile]
-        return carry
-
-    lax.fori_loop(0, nodes // cap, initial_step, 0)
-    loads[2].wait()
+        for offset in range(group):
+            initial[index * group + offset] = product[:, offset * tile : (offset + 1) * tile]
 
     def push(level, buffer):
         target = pushed_hbm.at[level] if level < layers else final_hbm
         return pltpu.make_async_copy(buffer.at[:, slice_rows(feat)], target, out_sem.at[level])
 
     states = [initial] + [ping if index % 2 == 0 else pong for index in range(layers)]
-    push(0, initial).start()
-    group = row_tiles // doms
 
     def layer_group(layer, index):
         beta = math.log(LAMBDA_DECAY / (layer + 1) + 1.0)
@@ -178,11 +183,11 @@
             row = index * group + offset
             picked = []
             for k in range(per_row):
-                column = columns_ref[row, k]
+                column = columns_ref[k, row]
                 if k < OWN_TILES:
                     picked.append(current[column])
                 else:
-                    picked.append(halo[column])
+                    picked.append(halo[jnp.maximum(column - row_tiles, 0)])
             total = lax.dot_general(
                 jnp.concatenate(picked, axis=1),
                 jnp.concatenate([values[row, k] for k in range(per_row)], axis=1),
@@ -202,42 +207,70 @@
         for offset in range(group):
             following[first + offset] = fresh[:, offset * tile : (offset + 1) * tile]
 
+    def arrive(level, step):
+        z_copy(level, step).wait_recv()
+        for hop in range(1, chips):
+            y_copy(level, step, hop).start()
+        c_copy(level, step, 0).start()
+
+    def relay(level, step):
+        for hop in range(1, chips):
+            y_copy(level, step, hop).wait_recv()
+            c_copy(level, step, hop).start()
+
     for level in range(layers + 1):
-        layer = level - 1
-        if layer >= 2:
-            push(layer - 1, states[layer - 1]).wait()
-        if layer >= 0:
-            layer_group(layer, 0)
-
-        def arrive(step, carry, level=level, layer=layer):
+        if level >= 3:
+            push(level - 2, states[level - 2]).wait()
+
+        def early(step, carry, level=level):
             if level < layers:
-                z_copy(level, step).wait_recv()
-                for hop in range(1, chips):
-                    y_copy(level, step, hop).start()
-                c_copy(level, step, 0).start()
-            if layer >= 0:
-                layer_group(layer, step)
+                arrive(level, step)
+            if level >= 1:
+                relay(level - 1, step + doms - 1 - LAG)
+            else:
+                initial_group(step)
+            if level >= 2:
+                layer_group(level - 2, step + doms - 2 - LAG)
             return carry
 
-        lax.fori_loop(1, doms, arrive, 0)
-        if layer >= 0:
-            push(layer + 1, states[layer + 1]).start()
-        if level < layers:
-
-            def relay(step, carry, level=level):
-                for hop in range(1, chips):
-                    y_copy(level, step, hop).wait_recv()
-                    c_copy(level, step, hop).start()
-                return carry
-
-            lax.fori_loop(1, doms, relay, 0)
+        lax.fori_loop(1, 1 + LAG, early, 0)
+        if level >= 2:
+            layer_group(level - 2, doms - 1)
+            push(level - 1, states[level - 1]).start()
+        if level >= 1:
 
             def settle(step, carry, level=level):
                 for hop in range(chips):
-                    c_copy(level, step, hop).wait_recv()
+                    c_copy(level - 1, step, hop).wait_recv()
                 return carry
 
             lax.fori_loop(1, doms, settle, 0)
+        else:
+            initial_group(0)
+        if level == 1:
+            loads[2].wait()
+
+        def late(step, carry, level=level):
+            if level < layers:
+                arrive(level, step)
+                relay(level, step - LAG)
+            if level == 0:
+                initial_group(step)
+            elif level < layers:
+                layer_group(level - 1, step - 1 - LAG)
+            return carry
+
+        if level < layers:
+            lax.fori_loop(1 + LAG, doms, late, 0)
+        if level == 0:
+            push(0, initial).start()
+
+    def last_step(index, carry):
+        layer_group(layers - 1, index)
+        return carry
+
+    lax.fori_loop(0, doms, last_step, 0)
+    push(layers, states[layers]).start()
 
     for step in range(1, feats):
         w_copy(step).wait_send()
@@ -302,7 +335,7 @@
             collective_id=0, has_side_effects=True, vmem_limit_bytes=67043328
         ),
     )(
-        jnp.where(jnp.arange(per_row) < OWN_TILES, tile_columns, tile_columns - row_tiles),
+        tile_columns.T,
         send_counts,
         send_rows[0],
         jnp.swapaxes(history, 1, 2).reshape(layers * width, nodes),

time: 91.7 us -> 91.2 us (level)
  the two profiles are of different devices: /device:TPU:9 before, /device:TPU:0 now
where the time goes in v2:
time: 91.2 us; the launch traced here: 91.1 us
  Pallas kernels  86.2 us (95%)
  local copies, waits for them, and re-layouts  4.16 us (5%)
    pallas_call x1, Pallas kernels, on_device(): pl.pallas_call(functools.partial(kernel, doms, feats, layers, tile), out_...  86.2 us
    reshape x1, local copies, waits for them, and re-layouts, on_device(): pushed = jnp.transpose(pushed, (0, 1, 3, 2)).reshape(layers, nodes, width)  3.29 us

profile of v2, /device:TPU:0, one launch (start us, length us, event | category | flops | bytes accessed | tf_op | source)
XLA Modules:
  0.0 91.1 jit_solution(15741758995654054536)
XLA Ops:
  0.6 86.2 %shard_map.95 = (bf16[4,32,64,128]{3,2,1,0:T(8,128)(2,1)}, bf16[32,64,128]{2,1,0:T(8,128)(2,1)}) custom-call(s32[6,32]{1,0:T(8,128)} %bitcast.21, s32[1,8]{1,0:T(1,128)} %counts_ref.1, s32[8,512]{1,0:T(8,128)} %bitcast.19, bf16[256,4096]{1,0:T(8,128)(2,1)} %bitcast.18, bf16[4096,128]{1,0:T(8,128)(2,1)} %features_hbm.1, bf16[64,128]{1,0:T(8,128)(2,1)} %bitcast.20, ...), custom_call_target="tpu_custom_call" | custom-call | tf_op jit(solution)/shard_map/pallas_call | solution.py:305
  86.9 0.0 copy-start
  86.9 3.3 %copy_bitcast_fusion = bf16[4,4096,64]{1,2,0:T(8,128)(2,1)} fusion(bf16[4,32,64,128]{3,2,1,0:T(8,128)(2,1)} %get-tuple-element.4), kind=kLoop, calls=%fused_computation | loop fusion | bytes 4194304 | tf_op jit(solution)/shard_map/reshape | solution.py:347
  90.2 0.0 copy-done
  90.2 0.9 copy_bitcast_fusion.1
Async XLA Ops:
  86.9 3.3 %copy-start = (bf16[32,64,128]{2,1,0:T(8,128)(2,1)S(1)}, bf16[32,64,128]{2,1,0:T(8,128)(2,1)}, u32[]{:S(2)}) copy-start(bf16[32,64,128]{2,1,0:T(8,128)(2,1)} %get-tuple-element.5) | copy-start | bytes 1572868

commit v3 on v2

--- a/solution.py
+++ b/solution.py
@@ -58,7 +58,7 @@
     blocks = cap // tile
 
     def partner(step):
-        flips, bit = doms - step, 1
+        flips, bit = lax.rem(step, 2) * (doms // 2) + step // 2, 1
         dest = dom
         while bit < doms:
             dest = dest + lax.rem(flips // bit, 2) * (bit - 2 * bit * lax.rem(dom // bit, 2))
@@ -141,14 +141,6 @@
         return carry
 
     lax.fori_loop(2, doms, gather_step, 0)
-    for level in range(1, layers):
-
-        def send_step(step, carry, level=level):
-            z_copy(level, step).start()
-            return carry
-
-        lax.fori_loop(1, doms, send_step, 0)
-
     for level in range(layers):
         halos[level][block_tiles(dom)] = jnp.zeros((blocks, width * feats, tile), jnp.bfloat16)
         weights_t[level] = weights_ref[level].astype(jnp.float32).T.astype(jnp.bfloat16)
@@ -209,6 +201,8 @@
 
     def arrive(level, step):
         z_copy(level, step).wait_recv()
+        if level + 1 < layers:
+            z_copy(level + 1, step).start()
         for hop in range(1, chips):
             y_copy(level, step, hop).start()
         c_copy(level, step, 0).start()

time: 91.2 us -> 79.8 us (0.87)
  Pallas kernels: 86.2 us -> 74.8 us
    pallas_call x1, Pallas kernels: 86.2 us -> 74.8 us  [on_device(): pl.pallas_call(functools.partial(kernel, doms, feats, layers, tile), out_...]
where the time goes in v3:
time: 79.8 us; the launch traced here: 79.6 us
  Pallas kernels  74.8 us (94%)
  local copies, waits for them, and re-layouts  4.16 us (5%)
    pallas_call x1, Pallas kernels, on_device(): pl.pallas_call(functools.partial(kernel, doms, feats, layers, tile), out_...  74.8 us
    reshape x1, local copies, waits for them, and re-layouts, on_device(): pushed = jnp.transpose(pushed, (0, 1, 3, 2)).reshape(layers, nodes, width)  3.29 us

profile of v3, /device:TPU:0, one launch (start us, length us, event | category | flops | bytes accessed | tf_op | source)
XLA Modules:
  0.0 79.6 jit_solution(7478473599669503881)
XLA Ops:
  0.6 74.8 %shard_map.95 = (bf16[4,32,64,128]{3,2,1,0:T(8,128)(2,1)}, bf16[32,64,128]{2,1,0:T(8,128)(2,1)}) custom-call(s32[6,32]{1,0:T(8,128)} %bitcast.21, s32[1,8]{1,0:T(1,128)} %counts_ref.1, s32[8,512]{1,0:T(8,128)} %bitcast.19, bf16[256,4096]{1,0:T(8,128)(2,1)} %bitcast.18, bf16[4096,128]{1,0:T(8,128)(2,1)} %features_hbm.1, bf16[64,128]{1,0:T(8,128)(2,1)} %bitcast.20, ...), custom_call_target="tpu_custom_call" | custom-call | tf_op jit(solution)/shard_map/pallas_call | solution.py:299
  75.5 0.0 copy-start
  75.5 3.3 %copy_bitcast_fusion = bf16[4,4096,64]{1,2,0:T(8,128)(2,1)} fusion(bf16[4,32,64,128]{3,2,1,0:T(8,128)(2,1)} %get-tuple-element.4), kind=kLoop, calls=%fused_computation | loop fusion | bytes 4194304 | tf_op jit(solution)/shard_map/reshape | solution.py:341
  78.8 0.0 copy-done
  78.8 0.9 %copy_bitcast_fusion.1 = bf16[4096,64]{0,1:T(8,128)(2,1)} fusion(bf16[32,64,128]{2,1,0:T(8,128)(2,1)S(1)} %copy-done), kind=kLoop, calls=%fused_computation.1 | loop fusion | bytes 1048576 | tf_op jit(solution)/shard_map/reshape | solution.py:342
Async XLA Ops:
  75.5 3.3 %copy-start = (bf16[32,64,128]{2,1,0:T(8,128)(2,1)S(1)}, bf16[32,64,128]{2,1,0:T(8,128)(2,1)}, u32[]{:S(2)}) copy-start(bf16[32,64,128]{2,1,0:T(8,128)(2,1)} %get-tuple-element.5) | copy-start | bytes 1572868
